TPU v7x, 32 devices: a whole 2x2x4 slice. The times are simulated.
32 devices in a mesh: group: 2 (over y), expert: 4 (over z), tensor: 2 (over core), section: 2 (over x).
Axes of the slice: x: 2, y: 2, z: 4, core: 2. Of those that a mesh axis runs over, the one named last changes fastest.
Arguments:
- tokens: bfloat16 [32, 2048], P(('group', 'expert')), parts along dimension 0, may hold values from -10 to 10
- lengths: int32 [32], P(('group', 'expert')), parts along dimension 0, may hold values from 1 to 256, as said below
- routes: int32 [2, 32, 2], P('section', ('group', 'expert')), parts along dimension 1, may hold values from 0 to 3, all different within a row
- attn_gain: float32 [2, 2048], P('section'), may hold values from 0.4 to 1.6
- w_qkv: bfloat16 [2, 2, 2048, 1536], P('section', 'tensor', None, 'expert'), may hold values from -0.5 to 0.5
- w_out: bfloat16 [2, 2048, 2048], P('section', 'tensor', 'expert'), may hold values from -0.125 to 0.125
- moe_gain: float32 [2, 2048], P('section'), may hold values from 0.4 to 1.6
- router: bfloat16 [2, 2048, 4], P('section'), may hold values from -0.125 to 0.125
- w_up: bfloat16 [2, 2048, 28672], P('section', None, ('expert', 'tensor')), may hold values from -0.125 to 0.125
- w_down: bfloat16 [2, 28672, 2048], P('section', ('expert', 'tensor')), may hold values from -0.0625 to 0.0625
- k_codes: int32 [2, 32, 16, 512], P('section', ('group', 'expert'), None, 'tensor'), parts along dimension 1, may hold values from -2147483648 to 2147483646
- k_scale: bfloat16 [2, 32, 8, 512], P('section', ('group', 'expert'), None, 'tensor'), parts along dimension 1, may hold values from 0.25 to 1
- k_zero: bfloat16 [2, 32, 8, 512], P('section', ('group', 'expert'), None, 'tensor'), parts along dimension 1, may hold values from -4 to 4
- v_codes: int32 [2, 32, 16, 512], P('section', ('group', 'expert'), None, 'tensor'), parts along dimension 1, may hold values from -2147483648 to 2147483646
- v_scale: bfloat16 [2, 32, 16, 256], P('section', ('group', 'expert'), 'tensor'), parts along dimension 1, may hold values from 0.25 to 1
- v_zero: bfloat16 [2, 32, 16, 256], P('section', ('group', 'expert'), 'tensor'), parts along dimension 1, may hold values from -4 to 4
Outputs:
- layer_outputs: bfloat16 [2, 32, 2048], P('section', ('group', 'expert')), parts along dimension 1
There are 2 independent parts, one for each index of `group`. A program takes and returns all parts, laid end to end along the dimension named above; an argument that names none is the same for every part. Nothing has to cross between parts.
Inputs may be any that keep to these rules, and one draw needn't show every extreme that they name: Each sequence has cached positions 0 to lengths - 1 and its new token stands at position lengths; some sequence has all 256. `routes`: the two experts of a token differ. `k_codes`: word w holds the codes of positions 16 * w to 16 * w + 15, position 16 * w + i in bits 2 * i and 2 * i + 1. `v_codes`: packed as the key codes.
All inputs are finite; a program needn't handle non-finite values.
Results may differ from a plain program's by a relative error of at most 0.015.
Values may be sent and summed in bfloat16 or wider, within the bound.
No kernel may reach another device: no remote copies, remote signals or barrier semaphores. Data moves between devices by JAX's collectives and lax.ppermute only.
A program may use at most 64 MiB of HBM per device.

v0:
```python
import math
import jax
import jax.numpy as jnp
from jax import lax
from jax.sharding import PartitionSpec as P

HEAD_DIM = 128
EXPERTS = 4
MB = 2
rope_base = 1000000.0
norm_eps = 1e-05


def passed_along(array, axis, by):
    count = lax.axis_size(axis)
    pairs = [(i, i + by) for i in range(count) if 0 <= i + by < count]
    return lax.ppermute(array, axis, pairs)


def rms_scale(values, gain_row):
    widened = values.astype(jnp.float32)
    return (
        widened
        * lax.rsqrt(jnp.mean(widened * widened, axis=-1, keepdims=True) + norm_eps)
        * gain_row
    )


def rotate(vector, angles):
    half_width = vector.shape[-1] // 2
    front_half = vector[..., :half_width]
    back_half = vector[..., half_width:]
    cosine_val = jnp.cos(angles)
    sine_val = jnp.sin(angles)
    return jnp.concatenate(
        [
            front_half * cosine_val - back_half * sine_val,
            back_half * cosine_val + front_half * sine_val,
        ],
        axis=-1,
    )


def unpack(packed):
    shifts = 2 * jnp.arange(16, dtype=jnp.int32)
    code_vals = jnp.bitwise_and(
        jnp.right_shift(packed[:, :, None, :], shifts[None, None, :, None]), 3
    )
    return code_vals.reshape(packed.shape[0], packed.shape[1] * 16, packed.shape[2])


def dequant_keys(packed, scales, zero_table):
    code_vals = unpack(packed).astype(jnp.float32)
    seq_count, positions, channels = code_vals.shape
    grouped = code_vals.reshape(seq_count, scales.shape[1], positions // scales.shape[1], channels)
    dequant = (
        grouped * scales.astype(jnp.float32)[:, :, None, :]
        + zero_table.astype(jnp.float32)[:, :, None, :]
    )
    return dequant.reshape(seq_count, positions, channels).astype(jnp.bfloat16)


def dequant_values(packed, scales, zero_table):
    code_vals = unpack(packed).astype(jnp.float32)
    seq_count, positions, channels = code_vals.shape
    groups = scales.shape[1]
    grouped = code_vals.reshape(seq_count, positions, groups, channels // groups)
    scale_turned = jnp.transpose(scales.astype(jnp.float32), (0, 2, 1))[:, :, :, None]
    zero_turned = jnp.transpose(zero_table.astype(jnp.float32), (0, 2, 1))[:, :, :, None]
    dequant = grouped * scale_turned + zero_turned
    return dequant.reshape(seq_count, positions, channels).astype(jnp.bfloat16)


def attend(queries, own_key, own_value, key_cache, value_cache, seq_lengths):
    scale_root = math.sqrt(queries.shape[-1])
    scores = (
        jnp.einsum("skrd,spkd->skrp", queries, key_cache, preferred_element_type=jnp.float32)
        / scale_root
    )
    own_score = (
        jnp.einsum("skrd,skd->skr", queries, own_key, preferred_element_type=jnp.float32)
        / scale_root
    )
    visible = (jnp.arange(key_cache.shape[1], dtype=jnp.int32)[None, :] < seq_lengths[:, None])[
        :, None, None, :
    ]
    highest = jnp.maximum(jnp.max(jnp.where(visible, scores, -1e30), axis=-1), own_score)
    exponents = jnp.where(visible, jnp.exp(scores - highest[..., None]), 0.0)
    own_exp = jnp.exp(own_score - highest)
    denominator = jnp.sum(exponents, axis=-1) + own_exp
    probabilities = (exponents / denominator[..., None]).astype(jnp.bfloat16)
    own_prob = (own_exp / denominator).astype(jnp.bfloat16)
    mixture = jnp.einsum(
        "skrp,spkd->skrd", probabilities, value_cache, preferred_element_type=jnp.float32
    )
    mixture = (
        mixture
        + own_prob.astype(jnp.float32)[..., None] * own_value.astype(jnp.float32)[:, :, None, :]
    )
    return mixture.astype(jnp.bfloat16).reshape(queries.shape[0], -1)


def per_device(
    tokens,
    lengths,
    routes,
    attn_gain,
    w_qkv,
    w_out,
    moe_gain,
    router,
    w_up,
    w_down,
    k_codes,
    k_scale,
    k_zero,
    v_codes,
    v_scale,
    v_zero,
):
    section_index = lax.axis_index("section")
    section_count = lax.axis_size("section")
    expert_devs = lax.axis_size("expert")
    group_size = expert_devs // EXPERTS
    seq_dev, model_width = tokens.shape
    per_block = seq_dev // MB
    kv_local = k_codes.shape[3] // HEAD_DIM
    q_local = w_out.shape[1] // HEAD_DIM
    group_ratio = q_local // kv_local
    qkv_weight = w_qkv[0, 0]
    out_weight = w_out[0]
    up_weight = w_up[0]
    down_weight = w_down[0]
    router_weight = router[0]
    attn_row = attn_gain[0]
    moe_row = moe_gain[0]
    frequency = jnp.power(rope_base, -2.0 * jnp.arange(HEAD_DIM // 2, dtype=jnp.float32) / HEAD_DIM)
    owner_expert = jnp.arange(expert_devs, dtype=jnp.int32) // group_size
    token_blocks = tokens.reshape(MB, per_block, model_width)
    incoming = jnp.zeros((per_block, model_width), jnp.bfloat16)
    results = jnp.zeros((MB, per_block, model_width), jnp.bfloat16)
    slot_ids = jnp.arange(MB, dtype=jnp.int32)
    total_ticks = MB + section_count - 1
    for tick_index in range(total_ticks):
        block_number = tick_index - section_index
        current_block = jnp.clip(block_number, 0, MB - 1)
        if tick_index < MB:
            fresh_rows = token_blocks[tick_index]
        else:
            fresh_rows = jnp.zeros_like(incoming)
        inputs = jnp.where(section_index == 0, fresh_rows, incoming)
        first_seq = current_block * per_block

        def take_rows(array_in):
            return lax.dynamic_slice_in_dim(array_in, first_seq, per_block, 0)

        seq_lengths = take_rows(lengths)
        route = take_rows(routes[0])
        normed = rms_scale(inputs, attn_row).astype(jnp.bfloat16)
        qkv_cols = jnp.dot(
            lax.all_gather(normed, "expert", axis=0, tiled=True),
            qkv_weight,
            preferred_element_type=jnp.float32,
        ).astype(jnp.bfloat16)
        qkv_rows = lax.all_to_all(qkv_cols, "expert", split_axis=0, concat_axis=1, tiled=True)
        queries = qkv_rows[:, : q_local * HEAD_DIM].reshape(
            per_block, kv_local, group_ratio, HEAD_DIM
        )
        new_keys = qkv_rows[:, q_local * HEAD_DIM : (q_local + kv_local) * HEAD_DIM].reshape(
            per_block, kv_local, HEAD_DIM
        )
        new_values = qkv_rows[:, (q_local + kv_local) * HEAD_DIM :].reshape(
            per_block, kv_local, HEAD_DIM
        )
        angles = seq_lengths.astype(jnp.float32)[:, None] * frequency[None, :]
        query_rot = rotate(queries.astype(jnp.float32), angles[:, None, None, :]).astype(
            jnp.bfloat16
        )
        key_rot = rotate(new_keys.astype(jnp.float32), angles[:, None, :]).astype(jnp.bfloat16)
        key_cache = dequant_keys(take_rows(k_codes[0]), take_rows(k_scale[0]), take_rows(k_zero[0]))
        value_cache = dequant_values(
            take_rows(v_codes[0]), take_rows(v_scale[0]), take_rows(v_zero[0])
        )
        positions = key_cache.shape[1]
        key_cache = key_cache.reshape(per_block, positions, kv_local, HEAD_DIM)
        value_cache = value_cache.reshape(per_block, positions, kv_local, HEAD_DIM)
        attended = attend(query_rot, key_rot, new_values, key_cache, value_cache, seq_lengths)
        out_cols = jnp.dot(
            lax.all_gather(attended, "expert", axis=0, tiled=True),
            out_weight,
            preferred_element_type=jnp.float32,
        )
        out_part = lax.all_to_all(out_cols, "expert", split_axis=0, concat_axis=1, tiled=True)
        out_full = lax.psum(out_part, "tensor")
        hidden = (inputs.astype(jnp.float32) + out_full).astype(jnp.bfloat16)
        moe_in = rms_scale(hidden, moe_row).astype(jnp.bfloat16)
        logits = jnp.dot(moe_in, router_weight, preferred_element_type=jnp.float32)
        chosen = route[:, :, None] == jnp.arange(EXPERTS, dtype=jnp.int32)[None, None, :]
        picked = jnp.sum(jnp.where(chosen, logits[:, None, :], 0.0), axis=-1)
        gate_first = 1.0 / (1.0 + jnp.exp(picked[:, 1] - picked[:, 0]))
        gate_second = 1.0 / (1.0 + jnp.exp(picked[:, 0] - picked[:, 1]))
        hit_first = route[None, :, 0] == owner_expert[:, None]
        hit_second = route[None, :, 1] == owner_expert[:, None]
        sending = jnp.where(
            (hit_first | hit_second)[:, :, None], moe_in[None, :, :], jnp.zeros((), jnp.bfloat16)
        )
        up_proj = jnp.einsum(
            "jcd,df->jcf",
            lax.all_to_all(sending, "expert", split_axis=0, concat_axis=0, tiled=True),
            up_weight,
            preferred_element_type=jnp.float32,
        )
        active = jax.nn.silu(up_proj).astype(jnp.bfloat16)
        partial_value = jnp.einsum(
            "jcf,fd->jcd", active, down_weight, preferred_element_type=jnp.float32
        ).astype(jnp.bfloat16)
        weight = jnp.where(hit_first, gate_first[None, :], 0.0) + jnp.where(
            hit_second, gate_second[None, :], 0.0
        )
        returned = lax.all_to_all(partial_value, "expert", split_axis=0, concat_axis=0, tiled=True)
        moe_part = jnp.sum(weight[:, :, None] * returned.astype(jnp.float32), axis=0)
        moe_out = lax.psum(moe_part, "tensor")
        output = (hidden.astype(jnp.float32) + moe_out).astype(jnp.bfloat16)
        keep_mask = (block_number >= 0) & (block_number < MB) & (slot_ids == current_block)
        results = jnp.where(keep_mask[:, None, None], output[None, :, :], results)
        if tick_index + 1 < total_ticks:
            incoming = passed_along(output, "section", 1)
    return results.reshape(1, seq_dev, model_width)


def solution(mesh):
    return jax.shard_map(
        per_device,
        mesh=mesh,
        in_specs=(
            P(("group", "expert"), None),
            P(("group", "expert")),
            P("section", ("group", "expert"), None),
            P("section", None),
            P("section", "tensor", None, "expert"),
            P("section", "tensor", "expert"),
            P("section", None),
            P("section", None, None),
            P("section", None, ("expert", "tensor")),
            P("section", ("expert", "tensor"), None),
            P("section", ("group", "expert"), None, "tensor"),
            P("section", ("group", "expert"), None, "tensor"),
            P("section", ("group", "expert"), None, "tensor"),
            P("section", ("group", "expert"), None, "tensor"),
            P("section", ("group", "expert"), "tensor", None),
            P("section", ("group", "expert"), "tensor", None),
        ),
        out_specs=P("section", ("group", "expert"), None),
        check_vma=False,
    )
```

profile of v0, /device:TPU:0, one launch (start us, length us, event | category | flops | bytes accessed | tf_op | source)
XLA Modules:
  0.0 329.7 jit_solution(4514468630163313030)
XLA Ops:
  1.9 14.9 %all-gather = bf16[4,2,2048]{2,1,0:T(2,128)(2,1)S(1)} all-gather(bf16[1,2,2048]{2,1,0:T(2,128)(2,1)S(1)} %fusion.149), channel_id=1, replica_groups=mesh['group'=2,'expert'=4,'tensor'=2,'section'=2] {'expert'}, dimensions={0}, use_global_device_ids=true | all-gather | bytes 40960 | tf_op jit(solution)/shard_map/all_gather | solution.py:161
  17.7 4.6 %all-to-all-start = ((bf16[4,2,384]{2,1,0:T(2,128)(2,1)}), bf16[4,2,384]{2,1,0:T(2,128)(2,1)S(1)}, u32[]{:S(2)}, u32[]{:S(2)}) async-start(bf16[4,2,384]{2,1,0:T(2,128)(2,1)} %all_to_all.96), calls=%async_computation | async-start | bytes 12288 | tf_op jit(solution)/shard_map/all_to_all | solution.py:165
  23.2 1.5 constant_dynamic-slice_fusion.2
  30.1 1.3 shift_right_arithmetic.152
  32.3 2.1 add.301
  35.2 2.1 mul.556
  38.9 2.1 shift_right_arithmetic.159
  41.9 2.1 copy.132
  44.8 2.0 copy.133
  48.6 1.6 select_reduce_fusion.2
  50.5 1.6 fusion.36
  52.1 13.8 %all-gather.1 = bf16[4,2,1024]{2,1,0:T(2,128)(2,1)S(1)} all-gather(bf16[1,2,1024]{2,1,0:T(2,128)(2,1)S(1)} %reshape.1245), channel_id=1, replica_groups=mesh['group'=2,'expert'=4,'tensor'=2,'section'=2] {'expert'}, dimensions={0}, use_global_device_ids=true | all-gather | bytes 20480 | tf_op jit(solution)/shard_map/all_gather | solution.py:189
  66.8 4.5 %all-to-all-start.1 = ((f32[4,2,512]{2,1,0:T(2,128)}), f32[4,2,512]{2,1,0:T(2,128)S(1)}, u32[]{:S(2)}, u32[]{:S(2)}) async-start(f32[4,2,512]{2,1,0:T(2,128)} %fusion.43), calls=%async_computation.1 | async-start | bytes 32768 | tf_op jit(solution)/shard_map/all_to_all | solution.py:193
  73.4 3.5 %all-to-all-done.1 = f32[4,2,512]{2,1,0:T(2,128)S(1)} async-done(((f32[4,2,512]{2,1,0:T(2,128)}), f32[4,2,512]{2,1,0:T(2,128)S(1)}, u32[]{:S(2)}, u32[]{:S(2)}) %all-to-all-start.1) | async-done | bytes 16416 | tf_op jit(solution)/shard_map/all_to_all | solution.py:193
  76.9 3.3 %psum.42 = f32[2,2048]{1,0:T(2,128)S(1)} all-reduce(f32[2,2048]{1,0:T(2,128)S(1)} %bitcast.222), channel_id=1, replica_groups=mesh['group'=2,'expert'=4,'tensor'=2,'section'=2] {'tensor'}, use_global_device_ids=true, to_apply=%region_3.4 | all-reduce | flops 4096 | bytes 32768 | tf_op jit(solution)/shard_map/psum | solution.py:194
  82.2 3.3 all-to-all-start.2
  85.7 5.4 %all-to-all-done.2 = bf16[4,2,2048]{2,1,0:T(2,128)(2,1)S(1)} async-done(((bf16[4,2,2048]{2,1,0:T(2,128)(2,1)}), bf16[4,2,2048]{2,1,0:T(2,128)(2,1)S(1)}, u32[]{:S(2)}, u32[]{:S(2)}) %all-to-all-start.2) | async-done | bytes 32800 | tf_op jit(solution)/shard_map/all_to_all | solution.py:209
  91.1 11.6 %fusion.12 = bf16[4,2,2048]{2,0,1:T(4,128)(2,1)S(1)} fusion(bf16[1,3584,2048]{2,1,0:T(8,128)(2,1)} %param.25, bf16[1,2048,3584]{2,1,0:T(8,128)(2,1)} %param.24, bf16[4,2,2048]{2,1,0:T(2,128)(2,1)S(1)} %all-to-all-done.2), kind=kOutput, calls=%fused_computation.12 | convolution fusion | flops 235040768 | bytes 29425664 | tf_op jit(solution)/shard_map/jcf,fd->jcd/dot_general | solution.py:214
  103.3 3.3 all-to-all-start.3
  106.6 5.6 %all-to-all-done.3 = bf16[4,2,2048]{2,1,0:T(2,128)(2,1)S(1)} async-done(((bf16[4,2,2048]{2,1,0:T(2,128)(2,1)}), bf16[4,2,2048]{2,1,0:T(2,128)(2,1)S(1)}, u32[]{:S(2)}, u32[]{:S(2)}) %all-to-all-start.3) | async-done | bytes 32800 | tf_op jit(solution)/shard_map/all_to_all | solution.py:220
  112.3 3.4 %psum.43 = f32[2,2048]{1,0:T(2,128)S(1)} all-reduce(f32[2,2048]{1,0:T(2,128)S(1)} %multiply_reduce_fusion.2), channel_id=1, replica_groups=mesh['group'=2,'expert'=4,'tensor'=2,'section'=2] {'tensor'}, use_global_device_ids=true, to_apply=%region_7.8 | all-reduce | flops 4096 | bytes 32768 | tf_op jit(solution)/shard_map/psum | solution.py:222
  115.7 3.4 %collective-permute-start = (bf16[2,2048]{1,0:T(2,128)(2,1)S(1)}, bf16[2,2048]{1,0:T(2,128)(2,1)S(1)}, u32[]{:S(2)}, u32[]{:S(2)}) collective-permute-start(bf16[2,2048]{1,0:T(2,128)(2,1)S(1)} %fusion.112), channel_id=1, source_target_pairs={{0,1},{2,3},{4,5},{6,7},{8,9},{10,11},{12,13},{14,15},{16,17},{18,... | collective-permute-start | bytes 24584 | tf_op jit(solution)/shard_map/ppermute | solution.py:17
  120.7 13.1 %all-gather.2 = bf16[4,2,2048]{2,1,0:T(2,128)(2,1)S(1)} all-gather(bf16[1,2,2048]{2,1,0:T(2,128)(2,1)S(1)} %fusion.148), channel_id=1, replica_groups=mesh['group'=2,'expert'=4,'tensor'=2,'section'=2] {'expert'}, dimensions={0}, use_global_device_ids=true | all-gather | bytes 40960 | tf_op jit(solution)/shard_map/all_gather | solution.py:161
  134.7 3.2 all-to-all-start.4
  138.8 1.3 shift_right_arithmetic.163
  141.0 2.1 add.320
  143.9 2.1 mul.593
  146.9 2.1 shift_right_arithmetic.167
  149.8 2.1 copy.143
  152.7 2.0 copy.144
  155.3 1.6 select_reduce_fusion.1
  157.1 1.6 fusion.37
  158.7 13.7 %all-gather.3 = bf16[4,2,1024]{2,1,0:T(2,128)(2,1)S(1)} all-gather(bf16[1,2,1024]{2,1,0:T(2,128)(2,1)S(1)} %reshape.1249), channel_id=1, replica_groups=mesh['group'=2,'expert'=4,'tensor'=2,'section'=2] {'expert'}, dimensions={0}, use_global_device_ids=true | all-gather | bytes 20480 | tf_op jit(solution)/shard_map/all_gather | solution.py:189
  173.3 4.5 %all-to-all-start.5 = ((f32[4,2,512]{2,1,0:T(2,128)}), f32[4,2,512]{2,1,0:T(2,128)S(1)}, u32[]{:S(2)}, u32[]{:S(2)}) async-start(f32[4,2,512]{2,1,0:T(2,128)} %fusion.41), calls=%async_computation.5 | async-start | bytes 32768 | tf_op jit(solution)/shard_map/all_to_all | solution.py:193
  177.9 5.6 %all-to-all-done.5 = f32[4,2,512]{2,1,0:T(2,128)S(1)} async-done(((f32[4,2,512]{2,1,0:T(2,128)}), f32[4,2,512]{2,1,0:T(2,128)S(1)}, u32[]{:S(2)}, u32[]{:S(2)}) %all-to-all-start.5) | async-done | bytes 16416 | tf_op jit(solution)/shard_map/all_to_all | solution.py:193
  183.5 3.3 %psum.44 = f32[2,2048]{1,0:T(2,128)S(1)} all-reduce(f32[2,2048]{1,0:T(2,128)S(1)} %bitcast.221), channel_id=1, replica_groups=mesh['group'=2,'expert'=4,'tensor'=2,'section'=2] {'tensor'}, use_global_device_ids=true, to_apply=%region_11.12 | all-reduce | flops 4096 | bytes 32768 | tf_op jit(solution)/shard_map/psum | solution.py:194
  188.8 3.4 %all-to-all-start.6 = ((bf16[4,2,2048]{2,1,0:T(2,128)(2,1)}), bf16[4,2,2048]{2,1,0:T(2,128)(2,1)S(1)}, u32[]{:S(2)}, u32[]{:S(2)}) async-start(bf16[4,2,2048]{2,1,0:T(2,128)(2,1)} %broadcast_select_fusion.1), calls=%async_computation.6 | async-start | bytes 65536 | tf_op jit(solution)/shard_map/all_to_all | solution.py:209
  192.4 5.2 %all-to-all-done.6 = bf16[4,2,2048]{2,1,0:T(2,128)(2,1)S(1)} async-done(((bf16[4,2,2048]{2,1,0:T(2,128)(2,1)}), bf16[4,2,2048]{2,1,0:T(2,128)(2,1)S(1)}, u32[]{:S(2)}, u32[]{:S(2)}) %all-to-all-start.6) | async-done | bytes 32800 | tf_op jit(solution)/shard_map/all_to_all | solution.py:209
  197.7 11.6 %fusion.15 = bf16[4,2,2048]{2,0,1:T(4,128)(2,1)S(1)} fusion(bf16[1,3584,2048]{2,1,0:T(8,128)(2,1)} %param.25, bf16[1,2048,3584]{2,1,0:T(8,128)(2,1)} %param.24, bf16[4,2,2048]{2,1,0:T(2,128)(2,1)S(1)} %all-to-all-done.6), kind=kOutput, calls=%fused_computation.13 | convolution fusion | flops 235040768 | bytes 29425664 | tf_op jit(solution)/shard_map/jcf,fd->jcd/dot_general | solution.py:214
  209.9 3.3 all-to-all-start.7
  213.2 5.6 %all-to-all-done.7 = bf16[4,2,2048]{2,1,0:T(2,128)(2,1)S(1)} async-done(((bf16[4,2,2048]{2,1,0:T(2,128)(2,1)}), bf16[4,2,2048]{2,1,0:T(2,128)(2,1)S(1)}, u32[]{:S(2)}, u32[]{:S(2)}) %all-to-all-start.7) | async-done | bytes 32800 | tf_op jit(solution)/shard_map/all_to_all | solution.py:220
  218.9 3.4 %psum.45 = f32[2,2048]{1,0:T(2,128)S(1)} all-reduce(f32[2,2048]{1,0:T(2,128)S(1)} %multiply_reduce_fusion.1), channel_id=1, replica_groups=mesh['group'=2,'expert'=4,'tensor'=2,'section'=2] {'tensor'}, use_global_device_ids=true, to_apply=%region_15.16 | all-reduce | flops 4096 | bytes 32768 | tf_op jit(solution)/shard_map/psum | solution.py:222
  222.3 4.2 %collective-permute-start.1 = (bf16[2,2048]{1,0:T(2,128)(2,1)S(1)}, bf16[2,2048]{1,0:T(2,128)(2,1)S(1)}, u32[]{:S(2)}, u32[]{:S(2)}) collective-permute-start(bf16[2,2048]{1,0:T(2,128)(2,1)S(1)} %fusion.120), channel_id=1, source_target_pairs={{0,1},{2,3},{4,5},{6,7},{8,9},{10,11},{12,13},{14,15},{16,17},{18,... | collective-permute-start | bytes 24584 | tf_op jit(solution)/shard_map/ppermute | solution.py:17
  226.5 1.3 collective-permute-done.1
  228.1 13.1 %all-gather.4 = bf16[4,2,2048]{2,1,0:T(2,128)(2,1)S(1)} all-gather(bf16[1,2,2048]{2,1,0:T(2,128)(2,1)S(1)} %fusion.147), channel_id=1, replica_groups=mesh['group'=2,'expert'=4,'tensor'=2,'section'=2] {'expert'}, dimensions={0}, use_global_device_ids=true | all-gather | bytes 40960 | tf_op jit(solution)/shard_map/all_gather | solution.py:161
  242.1 3.2 all-to-all-start.8
  246.2 1.3 shift_right_arithmetic.171
  248.4 2.1 add.339
  251.3 2.1 mul.628
  254.3 2.1 shift_right_arithmetic.175
  257.3 2.1 copy.154
  260.2 2.0 copy.155
  262.7 1.6 select_reduce_fusion
  264.5 1.6 fusion.38
  266.2 13.7 %all-gather.5 = bf16[4,2,1024]{2,1,0:T(2,128)(2,1)S(1)} all-gather(bf16[1,2,1024]{2,1,0:T(2,128)(2,1)S(1)} %reshape.1253), channel_id=1, replica_groups=mesh['group'=2,'expert'=4,'tensor'=2,'section'=2] {'expert'}, dimensions={0}, use_global_device_ids=true | all-gather | bytes 20480 | tf_op jit(solution)/shard_map/all_gather | solution.py:189
  280.8 4.5 %all-to-all-start.9 = ((f32[4,2,512]{2,1,0:T(2,128)}), f32[4,2,512]{2,1,0:T(2,128)S(1)}, u32[]{:S(2)}, u32[]{:S(2)}) async-start(f32[4,2,512]{2,1,0:T(2,128)} %fusion.39), calls=%async_computation.9 | async-start | bytes 32768 | tf_op jit(solution)/shard_map/all_to_all | solution.py:193
  285.9 5.0 %all-to-all-done.9 = f32[4,2,512]{2,1,0:T(2,128)S(1)} async-done(((f32[4,2,512]{2,1,0:T(2,128)}), f32[4,2,512]{2,1,0:T(2,128)S(1)}, u32[]{:S(2)}, u32[]{:S(2)}) %all-to-all-start.9) | async-done | bytes 16416 | tf_op jit(solution)/shard_map/all_to_all | solution.py:193
  290.9 3.3 %psum.46 = f32[2,2048]{1,0:T(2,128)S(1)} all-reduce(f32[2,2048]{1,0:T(2,128)S(1)} %bitcast.220), channel_id=1, replica_groups=mesh['group'=2,'expert'=4,'tensor'=2,'section'=2] {'tensor'}, use_global_device_ids=true, to_apply=%region_19.20 | all-reduce | flops 4096 | bytes 32768 | tf_op jit(solution)/shard_map/psum | solution.py:194
  295.5 3.3 all-to-all-start.10
  299.0 5.4 %all-to-all-done.10 = bf16[4,2,2048]{2,1,0:T(2,128)(2,1)S(1)} async-done(((bf16[4,2,2048]{2,1,0:T(2,128)(2,1)}), bf16[4,2,2048]{2,1,0:T(2,128)(2,1)S(1)}, u32[]{:S(2)}, u32[]{:S(2)}) %all-to-all-start.10) | async-done | bytes 32800 | tf_op jit(solution)/shard_map/all_to_all | solution.py:209
  304.4 11.6 %fusion.18 = bf16[4,2,2048]{2,0,1:T(4,128)(2,1)S(1)} fusion(bf16[1,3584,2048]{2,1,0:T(8,128)(2,1)} %param.25, bf16[1,2048,3584]{2,1,0:T(8,128)(2,1)} %param.24, bf16[4,2,2048]{2,1,0:T(2,128)(2,1)S(1)} %all-to-all-done.10), kind=kOutput, calls=%fused_computation.14 | convolution fusion | flops 235040768 | bytes 29425664 | tf_op jit(solution)/shard_map/jcf,fd->jcd/dot_general | solution.py:214
  316.6 3.3 all-to-all-start.11
  319.9 5.6 %all-to-all-done.11 = bf16[4,2,2048]{2,1,0:T(2,128)(2,1)S(1)} async-done(((bf16[4,2,2048]{2,1,0:T(2,128)(2,1)}), bf16[4,2,2048]{2,1,0:T(2,128)(2,1)S(1)}, u32[]{:S(2)}, u32[]{:S(2)}) %all-to-all-start.11) | async-done | bytes 32800 | tf_op jit(solution)/shard_map/all_to_all | solution.py:220
  325.6 3.4 %psum.47 = f32[2,2048]{1,0:T(2,128)S(1)} all-reduce(f32[2,2048]{1,0:T(2,128)S(1)} %multiply_reduce_fusion), channel_id=1, replica_groups=mesh['group'=2,'expert'=4,'tensor'=2,'section'=2] {'tensor'}, use_global_device_ids=true, to_apply=%region_23.24 | all-reduce | flops 4096 | bytes 32768 | tf_op jit(solution)/shard_map/psum | solution.py:222
  (174 shorter events, 45.4 us)
Async XLA Ops:
  0.0 16.7 %copy-start = (bf16[1,1,2048,384]{3,2,1,0:T(8,128)(2,1)S(1)}, bf16[1,1,2048,384]{3,2,1,0:T(8,128)(2,1)}, u32[]{:S(2)}) copy-start(bf16[1,1,2048,384]{3,2,1,0:T(8,128)(2,1)} %param.20) | copy-start | bytes 4718596
  0.0 80.2 %copy-start.4 = (bf16[4,2048]{1,0:T(4,128)(2,1)S(1)}, bf16[4,2048]{1,0:T(4,128)(2,1)}, u32[]{:S(2)}) copy-start(bf16[4,2048]{1,0:T(4,128)(2,1)} %param.16) | copy-start | bytes 49156
  0.0 65.9 %copy-start.1 = (bf16[1,1024,512]{2,1,0:T(8,128)(2,1)S(1)}, bf16[1,1024,512]{2,1,0:T(8,128)(2,1)}, u32[]{:S(2)}) copy-start(bf16[1,1024,512]{2,1,0:T(8,128)(2,1)} %param.21) | copy-start | bytes 3145732
  0.0 80.4 %copy-start.3 = (f32[1,2048]{1,0:T(1,128)S(1)}, f32[1,2048]{1,0:T(1,128)}, u32[]{:S(2)}) copy-start(f32[1,2048]{1,0:T(1,128)} %param.22) | copy-start | bytes 24580
  17.7 29.2 %all-to-all-start = ((bf16[4,2,384]{2,1,0:T(2,128)(2,1)}), bf16[4,2,384]{2,1,0:T(2,128)(2,1)S(1)}, u32[]{:S(2)}, u32[]{:S(2)}) async-start(bf16[4,2,384]{2,1,0:T(2,128)(2,1)} %all_to_all.96), calls=%async_computation | async-start | bytes 12288 | tf_op jit(solution)/shard_map/all_to_all | solution.py:165
  66.8 10.1 %all-to-all-start.1 = ((f32[4,2,512]{2,1,0:T(2,128)}), f32[4,2,512]{2,1,0:T(2,128)S(1)}, u32[]{:S(2)}, u32[]{:S(2)}) async-start(f32[4,2,512]{2,1,0:T(2,128)} %fusion.43), calls=%async_computation.1 | async-start | bytes 32768 | tf_op jit(solution)/shard_map/all_to_all | solution.py:193
  82.2 8.9 %all-to-all-start.2 = ((bf16[4,2,2048]{2,1,0:T(2,128)(2,1)}), bf16[4,2,2048]{2,1,0:T(2,128)(2,1)S(1)}, u32[]{:S(2)}, u32[]{:S(2)}) async-start(bf16[4,2,2048]{2,1,0:T(2,128)(2,1)} %broadcast_select_fusion.2), calls=%async_computation.2 | async-start | bytes 65536 | tf_op jit(solution)/shard_map/all_to_all | solution.py:209
  85.7 20.9 %copy-start.9 = (s32[2]{0:T(128)S(1)}, s32[2]{0:T(128)}, u32[]{:S(2)}) copy-start(s32[2]{0:T(128)} %get-tuple-element.11) | copy-start | bytes 28
  85.7 20.9 %copy-start.10 = (s32[2]{0:T(128)S(1)}, s32[2]{0:T(128)}, u32[]{:S(2)}) copy-start(s32[2]{0:T(128)} %get-tuple-element.12) | copy-start | bytes 28
  85.7 34.9 %copy-start.2 = (f32[1,2048]{1,0:T(1,128)S(1)}, f32[1,2048]{1,0:T(1,128)}, u32[]{:S(2)}) copy-start(f32[1,2048]{1,0:T(1,128)} %param.19) | copy-start | bytes 24580
  85.7 69.1 %copy-start.7 = (f32[2,64]{1,0:T(2,128)S(1)}, f32[2,64]{1,0:T(2,128)}, u32[]{:S(2)}) copy-start(f32[2,64]{1,0:T(2,128)} %get-tuple-element.82) | copy-start | bytes 1540
  85.7 69.1 %copy-start.8 = (f32[2,64]{1,0:T(2,128)S(1)}, f32[2,64]{1,0:T(2,128)}, u32[]{:S(2)}) copy-start(f32[2,64]{1,0:T(2,128)} %get-tuple-element.83) | copy-start | bytes 1540
  103.3 8.9 %all-to-all-start.3 = ((bf16[4,2,2048]{2,1,0:T(2,128)(2,1)}), bf16[4,2,2048]{2,1,0:T(2,128)(2,1)S(1)}, u32[]{:S(2)}, u32[]{:S(2)}) async-start(bf16[4,2,2048]{2,1,0:T(2,128)(2,1)} %copy.138), calls=%async_computation.3 | async-start | bytes 65536 | tf_op jit(solution)/shard_map/all_to_all | solution.py:220
  115.7 4.8 %collective-permute-start = (bf16[2,2048]{1,0:T(2,128)(2,1)S(1)}, bf16[2,2048]{1,0:T(2,128)(2,1)S(1)}, u32[]{:S(2)}, u32[]{:S(2)}) collective-permute-start(bf16[2,2048]{1,0:T(2,128)(2,1)S(1)} %fusion.112), channel_id=1, source_target_pairs={{0,1},{2,3},{4,5},{6,7},{8,9},{10,11},{12,13},{14,15},{16,17},{18,... | collective-permute-start | bytes 24584 | tf_op jit(solution)/shard_map/ppermute | solution.py:17
  134.7 20.1 %all-to-all-start.4 = ((bf16[4,2,384]{2,1,0:T(2,128)(2,1)}), bf16[4,2,384]{2,1,0:T(2,128)(2,1)S(1)}, u32[]{:S(2)}, u32[]{:S(2)}) async-start(bf16[4,2,384]{2,1,0:T(2,128)(2,1)} %all_to_all.105), calls=%async_computation.4 | async-start | bytes 12288 | tf_op jit(solution)/shard_map/all_to_all | solution.py:165
  173.3 10.1 %all-to-all-start.5 = ((f32[4,2,512]{2,1,0:T(2,128)}), f32[4,2,512]{2,1,0:T(2,128)S(1)}, u32[]{:S(2)}, u32[]{:S(2)}) async-start(f32[4,2,512]{2,1,0:T(2,128)} %fusion.41), calls=%async_computation.5 | async-start | bytes 32768 | tf_op jit(solution)/shard_map/all_to_all | solution.py:193
  188.8 8.9 %all-to-all-start.6 = ((bf16[4,2,2048]{2,1,0:T(2,128)(2,1)}), bf16[4,2,2048]{2,1,0:T(2,128)(2,1)S(1)}, u32[]{:S(2)}, u32[]{:S(2)}) async-start(bf16[4,2,2048]{2,1,0:T(2,128)(2,1)} %broadcast_select_fusion.1), calls=%async_computation.6 | async-start | bytes 65536 | tf_op jit(solution)/shard_map/all_to_all | solution.py:209
  192.4 69.8 %copy-start.5 = (f32[2,64]{1,0:T(2,128)S(1)}, f32[2,64]{1,0:T(2,128)}, u32[]{:S(2)}) copy-start(f32[2,64]{1,0:T(2,128)} %get-tuple-element.73) | copy-start | bytes 1540
  192.4 69.8 %copy-start.6 = (f32[2,64]{1,0:T(2,128)S(1)}, f32[2,64]{1,0:T(2,128)}, u32[]{:S(2)}) copy-start(f32[2,64]{1,0:T(2,128)} %get-tuple-element.74) | copy-start | bytes 1540
  209.2 85.2 %copy-start.11 = (bf16[1,2048,4]{1,2,0:T(4,128)(2,1)S(1)}, bf16[1,2048,4]{1,2,0:T(4,128)(2,1)}, u32[]{:S(2)}) copy-start(bf16[1,2048,4]{1,2,0:T(4,128)(2,1)} %param.23) | copy-start | bytes 49156
  209.9 8.9 %all-to-all-start.7 = ((bf16[4,2,2048]{2,1,0:T(2,128)(2,1)}), bf16[4,2,2048]{2,1,0:T(2,128)(2,1)S(1)}, u32[]{:S(2)}, u32[]{:S(2)}) async-start(bf16[4,2,2048]{2,1,0:T(2,128)(2,1)} %copy.149), calls=%async_computation.7 | async-start | bytes 65536 | tf_op jit(solution)/shard_map/all_to_all | solution.py:220
  222.3 5.6 %collective-permute-start.1 = (bf16[2,2048]{1,0:T(2,128)(2,1)S(1)}, bf16[2,2048]{1,0:T(2,128)(2,1)S(1)}, u32[]{:S(2)}, u32[]{:S(2)}) collective-permute-start(bf16[2,2048]{1,0:T(2,128)(2,1)S(1)} %fusion.120), channel_id=1, source_target_pairs={{0,1},{2,3},{4,5},{6,7},{8,9},{10,11},{12,13},{14,15},{16,17},{18,... | collective-permute-start | bytes 24584 | tf_op jit(solution)/shard_map/ppermute | solution.py:17
  242.1 20.1 %all-to-all-start.8 = ((bf16[4,2,384]{2,1,0:T(2,128)(2,1)}), bf16[4,2,384]{2,1,0:T(2,128)(2,1)S(1)}, u32[]{:S(2)}, u32[]{:S(2)}) async-start(bf16[4,2,384]{2,1,0:T(2,128)(2,1)} %all_to_all.114), calls=%async_computation.8 | async-start | bytes 12288 | tf_op jit(solution)/shard_map/all_to_all | solution.py:165
  280.8 10.1 %all-to-all-start.9 = ((f32[4,2,512]{2,1,0:T(2,128)}), f32[4,2,512]{2,1,0:T(2,128)S(1)}, u32[]{:S(2)}, u32[]{:S(2)}) async-start(f32[4,2,512]{2,1,0:T(2,128)} %fusion.39), calls=%async_computation.9 | async-start | bytes 32768 | tf_op jit(solution)/shard_map/all_to_all | solution.py:193
  295.5 8.9 %all-to-all-start.10 = ((bf16[4,2,2048]{2,1,0:T(2,128)(2,1)}), bf16[4,2,2048]{2,1,0:T(2,128)(2,1)S(1)}, u32[]{:S(2)}, u32[]{:S(2)}) async-start(bf16[4,2,2048]{2,1,0:T(2,128)(2,1)} %broadcast_select_fusion), calls=%async_computation.10 | async-start | bytes 65536 | tf_op jit(solution)/shard_map/all_to_all | solution.py:209
  316.6 8.9 %all-to-all-start.11 = ((bf16[4,2,2048]{2,1,0:T(2,128)(2,1)}), bf16[4,2,2048]{2,1,0:T(2,128)(2,1)S(1)}, u32[]{:S(2)}, u32[]{:S(2)}) async-start(bf16[4,2,2048]{2,1,0:T(2,128)(2,1)} %copy.160), calls=%async_computation.11 | async-start | bytes 65536 | tf_op jit(solution)/shard_map/all_to_all | solution.py:220
where the time goes:
time: 332 us; the launch traced here: 330 us
  blocking collectives  102 us (31%)
  local copies, waits for them, and re-layouts  60.5 us (18%)
  starting transfers between devices  52.1 us (16%)
  matrix products  50.3 us (15%)
  waiting for transfers between devices  49.4 us (15%)
  other arithmetic  14.4 us (4%)
    all_gather x3, blocking collectives, per_device(): lax.all_gather(attended, 'expert', axis=0, tiled=True)  41.2 us
    all_gather x3, blocking collectives, per_device(): lax.all_gather(normed, 'expert', axis=0, tiled=True)  41.1 us
    dot_general x3, matrix products, per_device(): jnp.einsum('jcf,fd->jcd', active, down_weight, preferred_element_type=jnp...  34.7 us
    shift_right_arithmetic x15, local copies, waits for them, and re-layouts, unpack(): jnp.right_shift(packed[:, :, None, :], shifts[None, None, :, None])  16.9 us
    all_to_all x3, waiting for transfers between devices, per_device(): lax.all_to_all(partial_value, 'expert', split_axis=0, concat_axis=0, tile...  16.8 us
    all_to_all x3, waiting for transfers between devices, per_device(): lax.all_to_all(sending, 'expert', split_axis=0, concat_axis=0, tiled=True)  16 us
    all_to_all x3, waiting for transfers between devices, per_device(): lax.all_to_all(out_cols, 'expert', split_axis=0, concat_axis=1, tiled=True)  14.1 us
    all_to_all x3, starting transfers between devices, per_device(): lax.all_to_all(out_cols, 'expert', split_axis=0, concat_axis=1, tiled=True)  13.6 us
  transfers between devices with their start and end apart: 14, of which 11 were waited for; matrix products, arithmetic and copies ran while one was open for 19% of the time, Pallas kernels for 0%

commit v1 on v0

--- a/solution.py
+++ b/solution.py
@@ -190,7 +190,12 @@
             out_weight,
             preferred_element_type=jnp.float32,
         )
-        out_part = lax.all_to_all(out_cols, "expert", split_axis=0, concat_axis=1, tiled=True)
+        out_part = jnp.concatenate(
+            lax.all_to_all(
+                jnp.stack(jnp.split(out_cols, lax.axis_size("expert"), axis=0)), "expert", 0, 0
+            ),
+            axis=1,
+        )
         out_full = lax.psum(out_part, "tensor")
         hidden = (inputs.astype(jnp.float32) + out_full).astype(jnp.bfloat16)
         moe_in = rms_scale(hidden, moe_row).astype(jnp.bfloat16)

time: 332 us -> 332 us (level)
  no operation moved by 1% of the time
where the time goes in v1:
time: 332 us; the launch traced here: 330 us
  blocking collectives  102 us (31%)
  local copies, waits for them, and re-layouts  60.6 us (18%)
  starting transfers between devices  52.1 us (16%)
  waiting for transfers between devices  49.4 us (15%)
  matrix products  48.4 us (15%)
  other arithmetic  16.3 us (5%)
    all_gather x3, blocking collectives, per_device(): lax.all_gather(attended, 'expert', axis=0, tiled=True)  41.2 us
    all_gather x3, blocking collectives, per_device(): lax.all_gather(normed, 'expert', axis=0, tiled=True)  41.1 us
    dot_general x3, matrix products, per_device(): jnp.einsum('jcf,fd->jcd', active, down_weight, preferred_element_type=jnp...  34.7 us
    shift_right_arithmetic x15, local copies, waits for them, and re-layouts, unpack(): jnp.right_shift(packed[:, :, None, :], shifts[None, None, :, None])  16.9 us
    all_to_all x3, waiting for transfers between devices, per_device(): lax.all_to_all(partial_value, 'expert', split_axis=0, concat_axis=0, tile...  16.8 us
    all_to_all x3, waiting for transfers between devices, per_device(): lax.all_to_all(sending, 'expert', split_axis=0, concat_axis=0, tiled=True)  16 us
    all_to_all x3, waiting for transfers between devices, per_device(): lax.all_to_all(jnp.stack(jnp.split(out_cols, lax.axis_size('expert'), axi...  14.1 us
    all_to_all x3, starting transfers between devices, per_device(): lax.all_to_all(jnp.stack(jnp.split(out_cols, lax.axis_size('expert'), axi...  13.6 us
  transfers between devices with their start and end apart: 14, of which 11 were waited for; matrix products, arithmetic and copies ran while one was open for 19% of the time, Pallas kernels for 0%

profile of v1, /device:TPU:0, one launch (start us, length us, event | category | flops | bytes accessed | tf_op | source)
XLA Modules:
  0.0 329.7 jit_solution(14290421640113036209)
XLA Ops:
  1.9 14.9 %all-gather = bf16[4,2,2048]{2,1,0:T(2,128)(2,1)S(1)} all-gather(bf16[1,2,2048]{2,1,0:T(2,128)(2,1)S(1)} %fusion.149), channel_id=1, replica_groups=mesh['group'=2,'expert'=4,'tensor'=2,'section'=2] {'expert'}, dimensions={0}, use_global_device_ids=true | all-gather | bytes 40960 | tf_op jit(solution)/shard_map/all_gather | solution.py:161
  17.7 4.6 %all-to-all-start = ((bf16[4,2,384]{2,1,0:T(2,128)(2,1)}), bf16[4,2,384]{2,1,0:T(2,128)(2,1)S(1)}, u32[]{:S(2)}, u32[]{:S(2)}) async-start(bf16[4,2,384]{2,1,0:T(2,128)(2,1)} %all_to_all.69), calls=%async_computation | async-start | bytes 12288 | tf_op jit(solution)/shard_map/all_to_all | solution.py:165
  23.2 1.5 constant_dynamic-slice_fusion.2
  30.1 1.3 shift_right_arithmetic.152
  32.3 2.1 add.301
  35.2 2.1 mul.556
  38.9 2.1 shift_right_arithmetic.159
  41.9 2.1 copy.108
  44.8 2.0 copy.109
  48.6 1.6 select_reduce_fusion.2
  50.5 1.6 fusion.36
  52.1 13.8 %all-gather.1 = bf16[4,2,1024]{2,1,0:T(2,128)(2,1)S(1)} all-gather(bf16[1,2,1024]{2,1,0:T(2,128)(2,1)S(1)} %reshape.1257), channel_id=1, replica_groups=mesh['group'=2,'expert'=4,'tensor'=2,'section'=2] {'expert'}, dimensions={0}, use_global_device_ids=true | all-gather | bytes 20480 | tf_op jit(solution)/shard_map/all_gather | solution.py:189
  66.8 4.5 %all-to-all-start.1 = ((f32[4,2,512]{2,1,0:T(2,128)}), f32[4,2,512]{2,1,0:T(2,128)S(1)}, u32[]{:S(2)}, u32[]{:S(2)}) async-start(f32[4,2,512]{2,1,0:T(2,128)} %pad_maximum_fusion), calls=%async_computation.1 | async-start | bytes 32768 | tf_op jit(solution)/shard_map/all_to_all | solution.py:194
  73.5 3.5 %all-to-all-done.1 = f32[4,2,512]{2,1,0:T(2,128)S(1)} async-done(((f32[4,2,512]{2,1,0:T(2,128)}), f32[4,2,512]{2,1,0:T(2,128)S(1)}, u32[]{:S(2)}, u32[]{:S(2)}) %all-to-all-start.1) | async-done | bytes 16416 | tf_op jit(solution)/shard_map/all_to_all | solution.py:194
  76.9 3.3 %psum.42 = f32[2,2048]{1,0:T(2,128)S(1)} all-reduce(f32[2,2048]{1,0:T(2,128)S(1)} %bitcast.245), channel_id=1, replica_groups=mesh['group'=2,'expert'=4,'tensor'=2,'section'=2] {'tensor'}, use_global_device_ids=true, to_apply=%region_3.4 | all-reduce | flops 4096 | bytes 32768 | tf_op jit(solution)/shard_map/psum | solution.py:199
  82.2 3.3 all-to-all-start.2
  85.7 5.4 %all-to-all-done.2 = bf16[4,2,2048]{2,1,0:T(2,128)(2,1)S(1)} async-done(((bf16[4,2,2048]{2,1,0:T(2,128)(2,1)}), bf16[4,2,2048]{2,1,0:T(2,128)(2,1)S(1)}, u32[]{:S(2)}, u32[]{:S(2)}) %all-to-all-start.2) | async-done | bytes 32800 | tf_op jit(solution)/shard_map/all_to_all | solution.py:214
  91.1 11.6 %fusion.12 = bf16[4,2,2048]{2,0,1:T(4,128)(2,1)S(1)} fusion(bf16[1,3584,2048]{2,1,0:T(8,128)(2,1)} %param.25, bf16[1,2048,3584]{2,1,0:T(8,128)(2,1)} %param.24, bf16[4,2,2048]{2,1,0:T(2,128)(2,1)S(1)} %all-to-all-done.2), kind=kOutput, calls=%fused_computation.12 | convolution fusion | flops 235040768 | bytes 29425664 | tf_op jit(solution)/shard_map/jcf,fd->jcd/dot_general | solution.py:219
  103.3 3.3 all-to-all-start.3
  106.6 5.6 %all-to-all-done.3 = bf16[4,2,2048]{2,1,0:T(2,128)(2,1)S(1)} async-done(((bf16[4,2,2048]{2,1,0:T(2,128)(2,1)}), bf16[4,2,2048]{2,1,0:T(2,128)(2,1)S(1)}, u32[]{:S(2)}, u32[]{:S(2)}) %all-to-all-start.3) | async-done | bytes 32800 | tf_op jit(solution)/shard_map/all_to_all | solution.py:225
  112.3 3.4 %psum.43 = f32[2,2048]{1,0:T(2,128)S(1)} all-reduce(f32[2,2048]{1,0:T(2,128)S(1)} %multiply_reduce_fusion.2), channel_id=1, replica_groups=mesh['group'=2,'expert'=4,'tensor'=2,'section'=2] {'tensor'}, use_global_device_ids=true, to_apply=%region_7.8 | all-reduce | flops 4096 | bytes 32768 | tf_op jit(solution)/shard_map/psum | solution.py:227
  115.7 3.4 %collective-permute-start = (bf16[2,2048]{1,0:T(2,128)(2,1)S(1)}, bf16[2,2048]{1,0:T(2,128)(2,1)S(1)}, u32[]{:S(2)}, u32[]{:S(2)}) collective-permute-start(bf16[2,2048]{1,0:T(2,128)(2,1)S(1)} %fusion.112), channel_id=1, source_target_pairs={{0,1},{2,3},{4,5},{6,7},{8,9},{10,11},{12,13},{14,15},{16,17},{18,... | collective-permute-start | bytes 24584 | tf_op jit(solution)/shard_map/ppermute | solution.py:17
  120.7 13.1 %all-gather.2 = bf16[4,2,2048]{2,1,0:T(2,128)(2,1)S(1)} all-gather(bf16[1,2,2048]{2,1,0:T(2,128)(2,1)S(1)} %fusion.148), channel_id=1, replica_groups=mesh['group'=2,'expert'=4,'tensor'=2,'section'=2] {'expert'}, dimensions={0}, use_global_device_ids=true | all-gather | bytes 40960 | tf_op jit(solution)/shard_map/all_gather | solution.py:161
  134.7 3.2 all-to-all-start.4
  138.8 1.3 shift_right_arithmetic.163
  141.0 2.1 add.320
  143.9 2.1 mul.593
  146.9 2.1 shift_right_arithmetic.167
  149.9 2.1 copy.117
  152.8 2.0 copy.118
  155.3 1.6 select_reduce_fusion.1
  157.1 1.6 fusion.37
  158.8 13.7 %all-gather.3 = bf16[4,2,1024]{2,1,0:T(2,128)(2,1)S(1)} all-gather(bf16[1,2,1024]{2,1,0:T(2,128)(2,1)S(1)} %reshape.1261), channel_id=1, replica_groups=mesh['group'=2,'expert'=4,'tensor'=2,'section'=2] {'expert'}, dimensions={0}, use_global_device_ids=true | all-gather | bytes 20480 | tf_op jit(solution)/shard_map/all_gather | solution.py:189
  173.4 4.5 %all-to-all-start.5 = ((f32[4,2,512]{2,1,0:T(2,128)}), f32[4,2,512]{2,1,0:T(2,128)S(1)}, u32[]{:S(2)}, u32[]{:S(2)}) async-start(f32[4,2,512]{2,1,0:T(2,128)} %pad_maximum_fusion.1), calls=%async_computation.5 | async-start | bytes 32768 | tf_op jit(solution)/shard_map/all_to_all | solution.py:194
  177.9 5.6 %all-to-all-done.5 = f32[4,2,512]{2,1,0:T(2,128)S(1)} async-done(((f32[4,2,512]{2,1,0:T(2,128)}), f32[4,2,512]{2,1,0:T(2,128)S(1)}, u32[]{:S(2)}, u32[]{:S(2)}) %all-to-all-start.5) | async-done | bytes 16416 | tf_op jit(solution)/shard_map/all_to_all | solution.py:194
  183.5 3.3 %psum.44 = f32[2,2048]{1,0:T(2,128)S(1)} all-reduce(f32[2,2048]{1,0:T(2,128)S(1)} %bitcast.244), channel_id=1, replica_groups=mesh['group'=2,'expert'=4,'tensor'=2,'section'=2] {'tensor'}, use_global_device_ids=true, to_apply=%region_11.12 | all-reduce | flops 4096 | bytes 32768 | tf_op jit(solution)/shard_map/psum | solution.py:199
  188.8 3.4 %all-to-all-start.6 = ((bf16[4,2,2048]{2,1,0:T(2,128)(2,1)}), bf16[4,2,2048]{2,1,0:T(2,128)(2,1)S(1)}, u32[]{:S(2)}, u32[]{:S(2)}) async-start(bf16[4,2,2048]{2,1,0:T(2,128)(2,1)} %broadcast_select_fusion.1), calls=%async_computation.6 | async-start | bytes 65536 | tf_op jit(solution)/shard_map/all_to_all | solution.py:214
  192.5 5.2 %all-to-all-done.6 = bf16[4,2,2048]{2,1,0:T(2,128)(2,1)S(1)} async-done(((bf16[4,2,2048]{2,1,0:T(2,128)(2,1)}), bf16[4,2,2048]{2,1,0:T(2,128)(2,1)S(1)}, u32[]{:S(2)}, u32[]{:S(2)}) %all-to-all-start.6) | async-done | bytes 32800 | tf_op jit(solution)/shard_map/all_to_all | solution.py:214
  197.7 11.6 %fusion.15 = bf16[4,2,2048]{2,0,1:T(4,128)(2,1)S(1)} fusion(bf16[1,3584,2048]{2,1,0:T(8,128)(2,1)} %param.25, bf16[1,2048,3584]{2,1,0:T(8,128)(2,1)} %param.24, bf16[4,2,2048]{2,1,0:T(2,128)(2,1)S(1)} %all-to-all-done.6), kind=kOutput, calls=%fused_computation.13 | convolution fusion | flops 235040768 | bytes 29425664 | tf_op jit(solution)/shard_map/jcf,fd->jcd/dot_general | solution.py:219
  209.9 3.3 all-to-all-start.7
  213.2 5.6 %all-to-all-done.7 = bf16[4,2,2048]{2,1,0:T(2,128)(2,1)S(1)} async-done(((bf16[4,2,2048]{2,1,0:T(2,128)(2,1)}), bf16[4,2,2048]{2,1,0:T(2,128)(2,1)S(1)}, u32[]{:S(2)}, u32[]{:S(2)}) %all-to-all-start.7) | async-done | bytes 32800 | tf_op jit(solution)/shard_map/all_to_all | solution.py:225
  218.9 3.4 %psum.45 = f32[2,2048]{1,0:T(2,128)S(1)} all-reduce(f32[2,2048]{1,0:T(2,128)S(1)} %multiply_reduce_fusion.1), channel_id=1, replica_groups=mesh['group'=2,'expert'=4,'tensor'=2,'section'=2] {'tensor'}, use_global_device_ids=true, to_apply=%region_15.16 | all-reduce | flops 4096 | bytes 32768 | tf_op jit(solution)/shard_map/psum | solution.py:227
  222.3 4.2 %collective-permute-start.1 = (bf16[2,2048]{1,0:T(2,128)(2,1)S(1)}, bf16[2,2048]{1,0:T(2,128)(2,1)S(1)}, u32[]{:S(2)}, u32[]{:S(2)}) collective-permute-start(bf16[2,2048]{1,0:T(2,128)(2,1)S(1)} %fusion.120), channel_id=1, source_target_pairs={{0,1},{2,3},{4,5},{6,7},{8,9},{10,11},{12,13},{14,15},{16,17},{18,... | collective-permute-start | bytes 24584 | tf_op jit(solution)/shard_map/ppermute | solution.py:17
  226.5 1.3 collective-permute-done.1
  228.1 13.1 %all-gather.4 = bf16[4,2,2048]{2,1,0:T(2,128)(2,1)S(1)} all-gather(bf16[1,2,2048]{2,1,0:T(2,128)(2,1)S(1)} %fusion.147), channel_id=1, replica_groups=mesh['group'=2,'expert'=4,'tensor'=2,'section'=2] {'expert'}, dimensions={0}, use_global_device_ids=true | all-gather | bytes 40960 | tf_op jit(solution)/shard_map/all_gather | solution.py:161
  242.2 3.2 all-to-all-start.8
  246.3 1.3 shift_right_arithmetic.171
  248.4 2.1 add.339
  251.4 2.1 mul.628
  254.3 2.1 shift_right_arithmetic.175
  257.3 2.1 copy.126
  260.2 2.0 copy.127
  262.7 1.6 select_reduce_fusion
  264.5 1.6 fusion.38
  266.2 13.7 %all-gather.5 = bf16[4,2,1024]{2,1,0:T(2,128)(2,1)S(1)} all-gather(bf16[1,2,1024]{2,1,0:T(2,128)(2,1)S(1)} %reshape.1265), channel_id=1, replica_groups=mesh['group'=2,'expert'=4,'tensor'=2,'section'=2] {'expert'}, dimensions={0}, use_global_device_ids=true | all-gather | bytes 20480 | tf_op jit(solution)/shard_map/all_gather | solution.py:189
  280.8 4.5 %all-to-all-start.9 = ((f32[4,2,512]{2,1,0:T(2,128)}), f32[4,2,512]{2,1,0:T(2,128)S(1)}, u32[]{:S(2)}, u32[]{:S(2)}) async-start(f32[4,2,512]{2,1,0:T(2,128)} %pad_maximum_fusion.2), calls=%async_computation.9 | async-start | bytes 32768 | tf_op jit(solution)/shard_map/all_to_all | solution.py:194
  285.9 5.0 %all-to-all-done.9 = f32[4,2,512]{2,1,0:T(2,128)S(1)} async-done(((f32[4,2,512]{2,1,0:T(2,128)}), f32[4,2,512]{2,1,0:T(2,128)S(1)}, u32[]{:S(2)}, u32[]{:S(2)}) %all-to-all-start.9) | async-done | bytes 16416 | tf_op jit(solution)/shard_map/all_to_all | solution.py:194
  291.0 3.3 %psum.46 = f32[2,2048]{1,0:T(2,128)S(1)} all-reduce(f32[2,2048]{1,0:T(2,128)S(1)} %bitcast.243), channel_id=1, replica_groups=mesh['group'=2,'expert'=4,'tensor'=2,'section'=2] {'tensor'}, use_global_device_ids=true, to_apply=%region_19.20 | all-reduce | flops 4096 | bytes 32768 | tf_op jit(solution)/shard_map/psum | solution.py:199
  295.5 3.3 all-to-all-start.10
  299.0 5.4 %all-to-all-done.10 = bf16[4,2,2048]{2,1,0:T(2,128)(2,1)S(1)} async-done(((bf16[4,2,2048]{2,1,0:T(2,128)(2,1)}), bf16[4,2,2048]{2,1,0:T(2,128)(2,1)S(1)}, u32[]{:S(2)}, u32[]{:S(2)}) %all-to-all-start.10) | async-done | bytes 32800 | tf_op jit(solution)/shard_map/all_to_all | solution.py:214
  304.4 11.6 %fusion.18 = bf16[4,2,2048]{2,0,1:T(4,128)(2,1)S(1)} fusion(bf16[1,3584,2048]{2,1,0:T(8,128)(2,1)} %param.25, bf16[1,2048,3584]{2,1,0:T(8,128)(2,1)} %param.24, bf16[4,2,2048]{2,1,0:T(2,128)(2,1)S(1)} %all-to-all-done.10), kind=kOutput, calls=%fused_computation.14 | convolution fusion | flops 235040768 | bytes 29425664 | tf_op jit(solution)/shard_map/jcf,fd->jcd/dot_general | solution.py:219
  316.6 3.3 all-to-all-start.11
  319.9 5.6 %all-to-all-done.11 = bf16[4,2,2048]{2,1,0:T(2,128)(2,1)S(1)} async-done(((bf16[4,2,2048]{2,1,0:T(2,128)(2,1)}), bf16[4,2,2048]{2,1,0:T(2,128)(2,1)S(1)}, u32[]{:S(2)}, u32[]{:S(2)}) %all-to-all-start.11) | async-done | bytes 32800 | tf_op jit(solution)/shard_map/all_to_all | solution.py:225
  325.6 3.4 %psum.47 = f32[2,2048]{1,0:T(2,128)S(1)} all-reduce(f32[2,2048]{1,0:T(2,128)S(1)} %multiply_reduce_fusion), channel_id=1, replica_groups=mesh['group'=2,'expert'=4,'tensor'=2,'section'=2] {'tensor'}, use_global_device_ids=true, to_apply=%region_23.24 | all-reduce | flops 4096 | bytes 32768 | tf_op jit(solution)/shard_map/psum | solution.py:227
  (183 shorter events, 45.4 us)
Async XLA Ops:
  0.0 16.7 %copy-start = (bf16[1,1,2048,384]{3,2,1,0:T(8,128)(2,1)S(1)}, bf16[1,1,2048,384]{3,2,1,0:T(8,128)(2,1)}, u32[]{:S(2)}) copy-start(bf16[1,1,2048,384]{3,2,1,0:T(8,128)(2,1)} %param.20) | copy-start | bytes 4718596
  0.0 80.3 %copy-start.4 = (bf16[4,2048]{1,0:T(4,128)(2,1)S(1)}, bf16[4,2048]{1,0:T(4,128)(2,1)}, u32[]{:S(2)}) copy-start(bf16[4,2048]{1,0:T(4,128)(2,1)} %param.16) | copy-start | bytes 49156
  0.0 65.9 %copy-start.1 = (bf16[1,1024,512]{2,1,0:T(8,128)(2,1)S(1)}, bf16[1,1024,512]{2,1,0:T(8,128)(2,1)}, u32[]{:S(2)}) copy-start(bf16[1,1024,512]{2,1,0:T(8,128)(2,1)} %param.21) | copy-start | bytes 3145732
  0.0 80.4 %copy-start.3 = (f32[1,2048]{1,0:T(1,128)S(1)}, f32[1,2048]{1,0:T(1,128)}, u32[]{:S(2)}) copy-start(f32[1,2048]{1,0:T(1,128)} %param.22) | copy-start | bytes 24580
  17.7 29.2 %all-to-all-start = ((bf16[4,2,384]{2,1,0:T(2,128)(2,1)}), bf16[4,2,384]{2,1,0:T(2,128)(2,1)S(1)}, u32[]{:S(2)}, u32[]{:S(2)}) async-start(bf16[4,2,384]{2,1,0:T(2,128)(2,1)} %all_to_all.69), calls=%async_computation | async-start | bytes 12288 | tf_op jit(solution)/shard_map/all_to_all | solution.py:165
  66.8 10.1 %all-to-all-start.1 = ((f32[4,2,512]{2,1,0:T(2,128)}), f32[4,2,512]{2,1,0:T(2,128)S(1)}, u32[]{:S(2)}, u32[]{:S(2)}) async-start(f32[4,2,512]{2,1,0:T(2,128)} %pad_maximum_fusion), calls=%async_computation.1 | async-start | bytes 32768 | tf_op jit(solution)/shard_map/all_to_all | solution.py:194
  82.2 8.9 %all-to-all-start.2 = ((bf16[4,2,2048]{2,1,0:T(2,128)(2,1)}), bf16[4,2,2048]{2,1,0:T(2,128)(2,1)S(1)}, u32[]{:S(2)}, u32[]{:S(2)}) async-start(bf16[4,2,2048]{2,1,0:T(2,128)(2,1)} %broadcast_select_fusion.2), calls=%async_computation.2 | async-start | bytes 65536 | tf_op jit(solution)/shard_map/all_to_all | solution.py:214
  85.7 20.9 %copy-start.9 = (s32[2]{0:T(128)S(1)}, s32[2]{0:T(128)}, u32[]{:S(2)}) copy-start(s32[2]{0:T(128)} %get-tuple-element.11) | copy-start | bytes 28
  85.7 20.9 %copy-start.10 = (s32[2]{0:T(128)S(1)}, s32[2]{0:T(128)}, u32[]{:S(2)}) copy-start(s32[2]{0:T(128)} %get-tuple-element.12) | copy-start | bytes 28
  85.7 34.9 %copy-start.2 = (f32[1,2048]{1,0:T(1,128)S(1)}, f32[1,2048]{1,0:T(1,128)}, u32[]{:S(2)}) copy-start(f32[1,2048]{1,0:T(1,128)} %param.19) | copy-start | bytes 24580
  85.7 69.1 %copy-start.7 = (f32[2,64]{1,0:T(2,128)S(1)}, f32[2,64]{1,0:T(2,128)}, u32[]{:S(2)}) copy-start(f32[2,64]{1,0:T(2,128)} %get-tuple-element.94) | copy-start | bytes 1540
  85.7 69.1 %copy-start.8 = (f32[2,64]{1,0:T(2,128)S(1)}, f32[2,64]{1,0:T(2,128)}, u32[]{:S(2)}) copy-start(f32[2,64]{1,0:T(2,128)} %get-tuple-element.95) | copy-start | bytes 1540
  103.3 8.9 %all-to-all-start.3 = ((bf16[4,2,2048]{2,1,0:T(2,128)(2,1)}), bf16[4,2,2048]{2,1,0:T(2,128)(2,1)S(1)}, u32[]{:S(2)}, u32[]{:S(2)}) async-start(bf16[4,2,2048]{2,1,0:T(2,128)(2,1)} %copy.112), calls=%async_computation.3 | async-start | bytes 65536 | tf_op jit(solution)/shard_map/all_to_all | solution.py:225
  115.7 4.8 %collective-permute-start = (bf16[2,2048]{1,0:T(2,128)(2,1)S(1)}, bf16[2,2048]{1,0:T(2,128)(2,1)S(1)}, u32[]{:S(2)}, u32[]{:S(2)}) collective-permute-start(bf16[2,2048]{1,0:T(2,128)(2,1)S(1)} %fusion.112), channel_id=1, source_target_pairs={{0,1},{2,3},{4,5},{6,7},{8,9},{10,11},{12,13},{14,15},{16,17},{18,... | collective-permute-start | bytes 24584 | tf_op jit(solution)/shard_map/ppermute | solution.py:17
  134.7 20.1 %all-to-all-start.4 = ((bf16[4,2,384]{2,1,0:T(2,128)(2,1)}), bf16[4,2,384]{2,1,0:T(2,128)(2,1)S(1)}, u32[]{:S(2)}, u32[]{:S(2)}) async-start(bf16[4,2,384]{2,1,0:T(2,128)(2,1)} %all_to_all.76), calls=%async_computation.4 | async-start | bytes 12288 | tf_op jit(solution)/shard_map/all_to_all | solution.py:165
  173.4 10.1 %all-to-all-start.5 = ((f32[4,2,512]{2,1,0:T(2,128)}), f32[4,2,512]{2,1,0:T(2,128)S(1)}, u32[]{:S(2)}, u32[]{:S(2)}) async-start(f32[4,2,512]{2,1,0:T(2,128)} %pad_maximum_fusion.1), calls=%async_computation.5 | async-start | bytes 32768 | tf_op jit(solution)/shard_map/all_to_all | solution.py:194
  188.8 8.9 %all-to-all-start.6 = ((bf16[4,2,2048]{2,1,0:T(2,128)(2,1)}), bf16[4,2,2048]{2,1,0:T(2,128)(2,1)S(1)}, u32[]{:S(2)}, u32[]{:S(2)}) async-start(bf16[4,2,2048]{2,1,0:T(2,128)(2,1)} %broadcast_select_fusion.1), calls=%async_computation.6 | async-start | bytes 65536 | tf_op jit(solution)/shard_map/all_to_all | solution.py:214
  192.5 69.8 %copy-start.5 = (f32[2,64]{1,0:T(2,128)S(1)}, f32[2,64]{1,0:T(2,128)}, u32[]{:S(2)}) copy-start(f32[2,64]{1,0:T(2,128)} %get-tuple-element.85) | copy-start | bytes 1540
  192.5 69.8 %copy-start.6 = (f32[2,64]{1,0:T(2,128)S(1)}, f32[2,64]{1,0:T(2,128)}, u32[]{:S(2)}) copy-start(f32[2,64]{1,0:T(2,128)} %get-tuple-element.86) | copy-start | bytes 1540
  209.3 85.2 %copy-start.11 = (bf16[1,2048,4]{1,2,0:T(4,128)(2,1)S(1)}, bf16[1,2048,4]{1,2,0:T(4,128)(2,1)}, u32[]{:S(2)}) copy-start(bf16[1,2048,4]{1,2,0:T(4,128)(2,1)} %param.23) | copy-start | bytes 49156
  209.9 8.9 %all-to-all-start.7 = ((bf16[4,2,2048]{2,1,0:T(2,128)(2,1)}), bf16[4,2,2048]{2,1,0:T(2,128)(2,1)S(1)}, u32[]{:S(2)}, u32[]{:S(2)}) async-start(bf16[4,2,2048]{2,1,0:T(2,128)(2,1)} %copy.121), calls=%async_computation.7 | async-start | bytes 65536 | tf_op jit(solution)/shard_map/all_to_all | solution.py:225
  222.3 5.6 %collective-permute-start.1 = (bf16[2,2048]{1,0:T(2,128)(2,1)S(1)}, bf16[2,2048]{1,0:T(2,128)(2,1)S(1)}, u32[]{:S(2)}, u32[]{:S(2)}) collective-permute-start(bf16[2,2048]{1,0:T(2,128)(2,1)S(1)} %fusion.120), channel_id=1, source_target_pairs={{0,1},{2,3},{4,5},{6,7},{8,9},{10,11},{12,13},{14,15},{16,17},{18,... | collective-permute-start | bytes 24584 | tf_op jit(solution)/shard_map/ppermute | solution.py:17
  242.2 20.1 %all-to-all-start.8 = ((bf16[4,2,384]{2,1,0:T(2,128)(2,1)}), bf16[4,2,384]{2,1,0:T(2,128)(2,1)S(1)}, u32[]{:S(2)}, u32[]{:S(2)}) async-start(bf16[4,2,384]{2,1,0:T(2,128)(2,1)} %all_to_all.83), calls=%async_computation.8 | async-start | bytes 12288 | tf_op jit(solution)/shard_map/all_to_all | solution.py:165
  280.8 10.1 %all-to-all-start.9 = ((f32[4,2,512]{2,1,0:T(2,128)}), f32[4,2,512]{2,1,0:T(2,128)S(1)}, u32[]{:S(2)}, u32[]{:S(2)}) async-start(f32[4,2,512]{2,1,0:T(2,128)} %pad_maximum_fusion.2), calls=%async_computation.9 | async-start | bytes 32768 | tf_op jit(solution)/shard_map/all_to_all | solution.py:194
  295.5 8.9 %all-to-all-start.10 = ((bf16[4,2,2048]{2,1,0:T(2,128)(2,1)}), bf16[4,2,2048]{2,1,0:T(2,128)(2,1)S(1)}, u32[]{:S(2)}, u32[]{:S(2)}) async-start(bf16[4,2,2048]{2,1,0:T(2,128)(2,1)} %broadcast_select_fusion), calls=%async_computation.10 | async-start | bytes 65536 | tf_op jit(solution)/shard_map/all_to_all | solution.py:214
  316.6 8.9 %all-to-all-start.11 = ((bf16[4,2,2048]{2,1,0:T(2,128)(2,1)}), bf16[4,2,2048]{2,1,0:T(2,128)(2,1)S(1)}, u32[]{:S(2)}, u32[]{:S(2)}) async-start(bf16[4,2,2048]{2,1,0:T(2,128)(2,1)} %copy.130), calls=%async_computation.11 | async-start | bytes 65536 | tf_op jit(solution)/shard_map/all_to_all | solution.py:225
